TPU v7x, 1024 devices: a whole 8x8x8 slice. The times are simulated.
1024 devices in a mesh: gx: 4 (over y_hi), gy: 16 (over y_lo, z), gz: 16 (over x, core).
Axes of the slice: x: 8, y: 8 (y_hi: 4, y_lo: 2; y = y_hi * 2 + y_lo), z: 8, core: 2. Of those that a mesh axis runs over, the one named last changes fastest.
Arguments:
- conserved: float32 [5, 32, 128, 2048], P(None, 'gx', 'gy', 'gz'), may hold values from -3 to 4, as said below
- sigma_guess: float32 [32, 128, 2048], P('gx', 'gy', 'gz'), may hold values from -30 to 30
Outputs:
- advanced: float32 [5, 32, 128, 2048], P(None, 'gx', 'gy', 'gz')
- sigma_field: float32 [32, 128, 2048], P('gx', 'gy', 'gz')
Inputs may be any that keep to these rules, and one draw needn't show every extreme that they name: `conserved`: component 0 (density) lies between 0.5 and 2, components 1 to 3 (momenta) between -3 and 3, component 4 (energy) between 1 and 4.
All inputs are finite; a program needn't handle non-finite values.
Results may differ from a plain program's by a relative error of at most 0.00002.
Values sent between devices are 32-bit elements; how exact they have to be, the bound alone decides.
A program may use at most 64 MiB of HBM per device.

v0:
```python
import jax
import jax.numpy as jnp
from jax import lax
from jax.sharding import PartitionSpec as P

SWEEPS = 4


ALPHA = 10.0
GAMMA = 1.4
LAMBDA = 3.0
STEP_DT = 0.4


def extended(cells, sides, width):
    for axis, dim in sides:
        count = lax.axis_size(axis)
        head = lax.slice_in_dim(cells, 0, width, axis=dim)
        tail = lax.slice_in_dim(cells, cells.shape[dim] - width, cells.shape[dim], axis=dim)
        cells = jnp.concatenate(
            [
                lax.ppermute(tail, axis, [(i, (i + 1) % count) for i in range(count)]),
                cells,
                lax.ppermute(head, axis, [((i + 1) % count, i) for i in range(count)]),
            ],
            axis=dim,
        )
    return cells


def trim_margin(field, margin):
    if margin == 0:
        return field
    return field[..., margin:-margin, margin:-margin, margin:-margin]


def central(field, direction):
    length = field.shape[direction]
    upper_part = lax.slice_in_dim(field, 2, length, axis=direction)
    lower_part = lax.slice_in_dim(field, 0, length - 2, axis=direction)
    slope = 0.5 * (upper_part - lower_part)
    for across in range(3):
        if across != direction:
            slope = lax.slice_in_dim(slope, 1, slope.shape[across] - 1, axis=across)
    return slope


def neighbour(field, direction, offset):
    length = field.shape[direction]
    moved = lax.slice_in_dim(field, 1 - offset, length - 1 - offset, axis=direction)
    for across in range(3):
        if across != direction:
            moved = lax.slice_in_dim(moved, 1, moved.shape[across] - 1, axis=across)
    return moved


def source_term(velocity):
    gradient = [[central(velocity[member], across) for across in range(3)] for member in range(3)]
    trace_sq = jnp.zeros_like(gradient[0][0])
    for member in range(3):
        for across in range(3):
            trace_sq = trace_sq + gradient[member][across] * gradient[across][member]
    divergence = gradient[0][0] + gradient[1][1] + gradient[2][2]
    return trace_sq + divergence * divergence


def jacobi_sweep(sigma_now, inv_density, source):
    centre = trim_margin(inv_density, 1)
    acc_num = jnp.zeros_like(centre)
    acc_den = jnp.zeros_like(centre)
    for direction in range(3):
        for offset in (1, -1):
            weight_face = 0.5 * (centre + neighbour(inv_density, direction, offset))
            acc_num = acc_num + weight_face * neighbour(sigma_now, direction, offset)
            acc_den = acc_den + weight_face
    return (ALPHA * source + ALPHA * acc_num) / (centre + ALPHA * acc_den)


def physical(states, sigma_face, direction):
    density = states[0]
    normal_speed = states[1 + direction] / density
    kinetic = (
        0.5 * (states[1] * states[1] + states[2] * states[2] + states[3] * states[3]) / density
    )
    pressure = (GAMMA - 1.0) * (states[4] - kinetic) + sigma_face
    flux_rows = [states[1 + direction]]
    for member in range(3):
        flux_term = states[1 + member] * normal_speed
        if member == direction:
            flux_term = flux_term + pressure
        flux_rows.append(flux_term)
    flux_rows.append((states[4] + pressure) * normal_speed)
    return jnp.stack(flux_rows)


def flux_change(padded_state, padded_sigma, direction):
    strip = padded_state
    sigma_strip = padded_sigma
    for across in range(3):
        if across != direction:
            strip = lax.slice_in_dim(strip, 2, strip.shape[across + 1] - 2, axis=across + 1)
            sigma_strip = lax.slice_in_dim(
                sigma_strip, 2, sigma_strip.shape[across] - 2, axis=across
            )
    span_len = sigma_strip.shape[direction] - 4

    def window(field, start, axis_at):
        return lax.slice_in_dim(field, start, start + span_len + 1, axis=axis_at)

    axis_q = direction + 1
    left_state = (
        5.0 * window(strip, 1, axis_q) + 2.0 * window(strip, 2, axis_q) - window(strip, 0, axis_q)
    ) / 6.0
    right_state = (
        2.0 * window(strip, 1, axis_q) + 5.0 * window(strip, 2, axis_q) - window(strip, 3, axis_q)
    ) / 6.0
    left_sigma = (
        5.0 * window(sigma_strip, 1, direction)
        + 2.0 * window(sigma_strip, 2, direction)
        - window(sigma_strip, 0, direction)
    ) / 6.0
    right_sigma = (
        2.0 * window(sigma_strip, 1, direction)
        + 5.0 * window(sigma_strip, 2, direction)
        - window(sigma_strip, 3, direction)
    ) / 6.0
    face_flux = 0.5 * (
        physical(left_state, left_sigma, direction) + physical(right_state, right_sigma, direction)
    ) - 0.5 * LAMBDA * (right_state - left_state)
    return lax.slice_in_dim(face_flux, 1, span_len + 1, axis=axis_q) - lax.slice_in_dim(
        face_flux, 0, span_len, axis=axis_q
    )


def on_device(conserved, sigma_guess):
    packed = jnp.concatenate([conserved, sigma_guess[None]], axis=0)
    wide_rim = extended(packed, (("gx", 1), ("gy", 2), ("gz", 3)), SWEEPS + 2)
    fields = wide_rim[:5]
    inv_density = 1.0 / fields[0]
    velocity = fields[1:4] / fields[0]
    source = source_term(velocity)
    sigma_now = wide_rim[5]
    for sweep_no in range(SWEEPS):
        sigma_now = jacobi_sweep(
            sigma_now, trim_margin(inv_density, sweep_no), trim_margin(source, sweep_no)
        )
    padded_state = trim_margin(fields, SWEEPS)
    sigma_field = trim_margin(sigma_now, 2)
    tendency = jnp.zeros_like(conserved)
    for direction in range(3):
        tendency = tendency - flux_change(padded_state, sigma_now, direction)
    advanced = conserved + STEP_DT * tendency
    return (advanced, sigma_field)


def solution(mesh):
    in_specs = (P(None, "gx", "gy", "gz"), P("gx", "gy", "gz"))
    out_specs = (P(None, "gx", "gy", "gz"), P("gx", "gy", "gz"))
    return jax.shard_map(
        on_device, mesh=mesh, in_specs=in_specs, out_specs=out_specs, check_vma=False
    )
```

profile of v0, /device:TPU:32, one launch (start us, length us, event | category | flops | bytes accessed | tf_op | source)
XLA Modules:
  0.0 108.9 jit_solution(11905965882797320374)
XLA Ops:
  0.6 1.0 fusion.84
  1.6 5.9 %collective-permute-start = (f32[6,6,8,128]{3,2,1,0:T(8,128)S(1)}, f32[6,6,8,128]{3,2,1,0:T(8,128)S(1)}, u32[]{:S(2)}, u32[]{:S(2)}) collective-permute-start(f32[6,6,8,128]{3,2,1,0:T(8,128)S(1)} %get-tuple-element.56), channel_id=1, source_target_pairs={{0,256},{256,512},{512,768},{768,0},{1,257},{257,513},{513,769},{7... | collective-permute-start | bytes 442376 | tf_op jit(solution)/shard_map/ppermute | solution.py:22
  7.6 10.6 %collective-permute-start.1 = (f32[6,6,8,128]{3,2,1,0:T(8,128)S(1)}, f32[6,6,8,128]{3,2,1,0:T(8,128)S(1)}, u32[]{:S(2)}, u32[]{:S(2)}) collective-permute-start(f32[6,6,8,128]{3,2,1,0:T(8,128)S(1)} %get-tuple-element.57), channel_id=1, source_target_pairs={{256,0},{512,256},{768,512},{0,768},{257,1},{513,257},{769,513},{1... | collective-permute-start | bytes 442376 | tf_op jit(solution)/shard_map/ppermute | solution.py:24
  18.2 1.2 %collective-permute-done = f32[6,6,8,128]{3,2,1,0:T(8,128)S(1)} collective-permute-done((f32[6,6,8,128]{3,2,1,0:T(8,128)S(1)}, f32[6,6,8,128]{3,2,1,0:T(8,128)S(1)}, u32[]{:S(2)}, u32[]{:S(2)}) %collective-permute-start) | collective-permute-done | bytes 147488 | tf_op jit(solution)/shard_map/ppermute | solution.py:22
  19.4 1.5 %collective-permute-done.1 = f32[6,6,8,128]{3,2,1,0:T(8,128)S(1)} collective-permute-done((f32[6,6,8,128]{3,2,1,0:T(8,128)S(1)}, f32[6,6,8,128]{3,2,1,0:T(8,128)S(1)}, u32[]{:S(2)}, u32[]{:S(2)}) %collective-permute-start.1) | collective-permute-done | bytes 147488 | tf_op jit(solution)/shard_map/ppermute | solution.py:24
  20.9 1.0 pad_maximum_fusion.2
  21.9 5.5 %copy.36 = f32[6,20,8,128]{2,1,3,0:T(8,128)} copy(f32[6,20,8,128]{3,2,1,0:T(8,128)S(1)} %pad_maximum_fusion.2) | data formatting | bytes 983040 | tf_op jit(solution)/shard_map/concatenate | solution.py:20
  27.5 4.0 %collective-permute-start.2 = (f32[6,20,6,128]{3,1,2,0:T(8,128)S(1)}, f32[6,20,6,128]{3,1,2,0:T(8,128)S(1)}, u32[]{:S(2)}, u32[]{:S(2)}) collective-permute-start(f32[6,20,6,128]{3,1,2,0:T(8,128)S(1)} %copy.47), channel_id=1, source_target_pairs={{0,16},{16,32},{32,48},{48,64},{64,80},{80,96},{96,112},{112,128},... | collective-permute-start | bytes 1105928 | tf_op jit(solution)/shard_map/ppermute | solution.py:22
  31.6 14.0 %collective-permute-start.3 = (f32[6,20,6,128]{3,1,2,0:T(8,128)S(1)}, f32[6,20,6,128]{3,1,2,0:T(8,128)S(1)}, u32[]{:S(2)}, u32[]{:S(2)}) collective-permute-start(f32[6,20,6,128]{3,1,2,0:T(8,128)S(1)} %copy.48), channel_id=1, source_target_pairs={{16,0},{32,16},{48,32},{64,48},{80,64},{96,80},{112,96},{128,112},... | collective-permute-start | bytes 1105928 | tf_op jit(solution)/shard_map/ppermute | solution.py:24
  45.7 0.7 copy-done.5
  46.4 0.6 constant_dynamic-update-slice_fusion.4
  47.0 0.6 constant_dynamic-update-slice_fusion.9
  47.6 6.2 %collective-permute-done.2 = f32[6,20,6,128]{3,1,2,0:T(8,128)S(1)} collective-permute-done((f32[6,20,6,128]{3,1,2,0:T(8,128)S(1)}, f32[6,20,6,128]{3,1,2,0:T(8,128)S(1)}, u32[]{:S(2)}, u32[]{:S(2)}) %collective-permute-start.2) | collective-permute-done | bytes 368672 | tf_op jit(solution)/shard_map/ppermute | solution.py:22
  53.8 5.6 %copy.35 = f32[6,20,6,128]{2,1,3,0:T(8,128)} copy(f32[6,20,6,128]{3,1,2,0:T(8,128)S(1)} %collective-permute-done.2) | data formatting | bytes 737280 | tf_op jit(solution)/shard_map/ppermute | solution.py:22
  59.5 5.6 %copy.37 = f32[6,20,6,128]{2,1,3,0:T(8,128)} copy(f32[6,20,6,128]{3,1,2,0:T(8,128)S(1)} %collective-permute-done.3) | data formatting | bytes 737280 | tf_op jit(solution)/shard_map/ppermute | solution.py:24
  65.1 11.1 %pad_maximum_fusion = f32[6,20,20,128]{2,1,3,0:T(8,128)S(1)} fusion(f32[6,20,6,128]{2,1,3,0:T(8,128)} %copy.37, f32[6,20,8,128]{2,1,3,0:T(8,128)} %copy.36, f32[6,20,6,128]{2,1,3,0:T(8,128)} %copy.35), kind=kLoop, calls=%fused_computation | loop fusion | flops 614400 | bytes 2457600 | tf_op jit(solution)/shard_map/concatenate | solution.py:20
  76.2 0.9 fusion.133
  77.1 3.0 %collective-permute-start.5 = (f32[6,20,20,6]{2,1,3,0:T(8,128)}, f32[6,20,20,6]{2,1,3,0:T(8,128)}, u32[]{:S(2)}, u32[]{:S(2)}) collective-permute-start(f32[6,20,20,6]{2,1,3,0:T(8,128)} %get-tuple-element.21), channel_id=1, source_target_pairs={{1,0},{2,1},{3,2},{4,3},{5,4},{6,5},{7,6},{8,7},{9,8},{10,9},{11,1... | collective-permute-start | bytes 172808 | tf_op jit(solution)/shard_map/ppermute | solution.py:24
  80.2 0.1 fusion.32
  80.4 0.1 fusion.34
  80.6 0.7 constant_dynamic-update-slice_fusion.10
  81.3 0.6 multiply_dynamic-update-slice_fusion.7
  82.0 6.4 %copy.39 = f32[6,20,20,128]{3,2,1,0:T(8,128)S(1)} copy(f32[6,20,20,128]{2,1,3,0:T(8,128)} %copy-done.1) | data formatting | bytes 2457600 | tf_op jit(solution)/shard_map/concatenate | solution.py:20
  88.4 1.9 %copy.38 = f32[6,20,20,6]{3,2,1,0:T(8,128)S(1)} copy(f32[6,20,20,6]{2,1,3,0:T(8,128)} %collective-permute-done.4) | data formatting | bytes 115200 | tf_op jit(solution)/shard_map/ppermute | solution.py:22
  90.2 3.0 %copy.40 = f32[6,20,20,6]{3,2,1,0:T(8,128)} copy(f32[6,20,20,6]{2,1,3,0:T(8,128)} %collective-permute-done.5) | data formatting | bytes 115200 | tf_op jit(solution)/shard_map/ppermute | solution.py:24
  93.2 2.7 %pad_maximum_fusion.1 = f32[6,20,20,140]{3,2,1,0:T(8,128)S(1)} fusion(f32[6,20,20,6]{3,2,1,0:T(8,128)} %copy.40, f32[6,20,20,128]{3,2,1,0:T(8,128)S(1)} %copy.39, f32[6,20,20,6]{3,2,1,0:T(8,128)S(1)} %copy.38), kind=kLoop, calls=%fused_computation.1 | loop fusion | flops 672000 | bytes 2688000 | tf_op jit(solution)/shard_map/concatenate | solution.py:20
  95.9 0.3 broadcast_divide_fusion
  96.2 0.2 slice_divide_fusion
  96.4 0.1 slice_bitcast_fusion.2
  96.5 0.2 fusion.135
  96.8 0.2 fusion.137
  97.1 0.2 fusion.139
  97.3 0.1 fusion.26
  97.4 0.4 maximum_bitcast_fusion.3
  97.8 0.3 maximum_bitcast_fusion
  98.1 0.5 fusion.30
  98.6 2.4 %fusion.3 = (f32[18,18,138]{2,1,0:T(8,128)S(1)}, f32[18,18,138]{2,1,0:T(8,128)S(1)}) fusion(f32[20,20,140]{2,1,0:T(8,128)S(1)} %maximum_bitcast_fusion, f32[18,20,140]{2,1,0:T(8,128)S(1)} %get-tuple-element.23, f32[18,20,140]{2,1,0:T(8,128)S(1)} %get-tuple-element.22, f32[20,20,140]{2,1,0:T(8,128)S(1)} %get-tuple-element.18, ...), kind=kLoop, calls=%fused_computation.13 | loop fusion | flops 2816856 | bytes 5365440 | tf_op jit(solution)/shard_map/div | solution.py:76
  100.9 1.0 fusion.38
  101.9 0.8 fusion.52
  102.8 0.7 fusion.66
  103.6 0.7 slice.1171
  104.3 0.1 constant_dynamic-update-slice_fusion.8
  104.5 0.8 bitcast_dynamic-update-slice_fusion.5
  105.2 0.6 multiply_dynamic-update-slice_fusion.6
  106.1 0.7 bitcast_dynamic-update-slice_fusion.4
  106.8 1.1 multiply_subtract_fusion.1
  107.9 0.1 bitcast_dynamic-update-slice_fusion.1
  108.1 0.8 fusion.81
  (58 shorter events, 1.3 us)
Async XLA Ops:
  1.6 17.8 %collective-permute-start = (f32[6,6,8,128]{3,2,1,0:T(8,128)S(1)}, f32[6,6,8,128]{3,2,1,0:T(8,128)S(1)}, u32[]{:S(2)}, u32[]{:S(2)}) collective-permute-start(f32[6,6,8,128]{3,2,1,0:T(8,128)S(1)} %get-tuple-element.56), channel_id=1, source_target_pairs={{0,256},{256,512},{512,768},{768,0},{1,257},{257,513},{513,769},{7... | collective-permute-start | bytes 442376 | tf_op jit(solution)/shard_map/ppermute | solution.py:22
  7.6 13.3 %collective-permute-start.1 = (f32[6,6,8,128]{3,2,1,0:T(8,128)S(1)}, f32[6,6,8,128]{3,2,1,0:T(8,128)S(1)}, u32[]{:S(2)}, u32[]{:S(2)}) collective-permute-start(f32[6,6,8,128]{3,2,1,0:T(8,128)S(1)} %get-tuple-element.57), channel_id=1, source_target_pairs={{256,0},{512,256},{768,512},{0,768},{257,1},{513,257},{769,513},{1... | collective-permute-start | bytes 442376 | tf_op jit(solution)/shard_map/ppermute | solution.py:24
  27.4 18.1 %copy-start.4 = (f32[5,8,8,128]{3,2,1,0:T(8,128)S(1)}, f32[5,8,8,128]{3,2,1,0:T(8,128)}, u32[]{:S(2)}) copy-start(f32[5,8,8,128]{3,2,1,0:T(8,128)} %param.2) | copy-start | bytes 491524
  27.4 18.1 %copy-start.9 = (f32[8,8,128]{2,1,0:T(8,128)S(1)}, f32[8,8,128]{2,1,0:T(8,128)}, u32[]{:S(2)}) copy-start(f32[8,8,128]{2,1,0:T(8,128)} %param.3) | copy-start | bytes 98308
  27.5 26.3 %collective-permute-start.2 = (f32[6,20,6,128]{3,1,2,0:T(8,128)S(1)}, f32[6,20,6,128]{3,1,2,0:T(8,128)S(1)}, u32[]{:S(2)}, u32[]{:S(2)}) collective-permute-start(f32[6,20,6,128]{3,1,2,0:T(8,128)S(1)} %copy.47), channel_id=1, source_target_pairs={{0,16},{16,32},{32,48},{48,64},{64,80},{80,96},{96,112},{112,128},... | collective-permute-start | bytes 1105928 | tf_op jit(solution)/shard_map/ppermute | solution.py:22
  31.6 27.9 %collective-permute-start.3 = (f32[6,20,6,128]{3,1,2,0:T(8,128)S(1)}, f32[6,20,6,128]{3,1,2,0:T(8,128)S(1)}, u32[]{:S(2)}, u32[]{:S(2)}) collective-permute-start(f32[6,20,6,128]{3,1,2,0:T(8,128)S(1)} %copy.48), channel_id=1, source_target_pairs={{16,0},{32,16},{48,32},{64,48},{80,64},{96,80},{112,96},{128,112},... | collective-permute-start | bytes 1105928 | tf_op jit(solution)/shard_map/ppermute | solution.py:24
  45.7 0.7 copy-start.5
  45.7 1.3 %copy-start.7 = (f32[5,9,8,128]{3,2,1,0:T(8,128)}, f32[5,9,8,128]{3,2,1,0:T(8,128)S(1)}, u32[]{:S(2)}) copy-start(f32[5,9,8,128]{3,2,1,0:T(8,128)S(1)} %get-tuple-element.33) | copy-start | bytes 552964
  76.2 5.1 %copy-start.1 = (f32[6,20,20,128]{2,1,3,0:T(8,128)}, f32[6,20,20,128]{2,1,3,0:T(8,128)S(1)}, u32[]{:S(2)}) copy-start(f32[6,20,20,128]{2,1,3,0:T(8,128)S(1)} %pad_maximum_fusion) | copy-start | bytes 3686404
  77.1 11.3 %collective-permute-start.4 = (f32[6,20,20,6]{2,1,3,0:T(8,128)S(1)}, f32[6,20,20,6]{2,1,3,0:T(8,128)}, u32[]{:S(2)}, u32[]{:S(2)}) collective-permute-start(f32[6,20,20,6]{2,1,3,0:T(8,128)S(1)} %get-tuple-element.20), channel_id=1, source_target_pairs={{0,1},{1,2},{2,3},{3,4},{4,5},{5,6},{6,7},{7,8},{8,9},{9,10},{10,1... | collective-permute-start | bytes 172808 | tf_op jit(solution)/shard_map/ppermute | solution.py:22
  77.1 13.1 %collective-permute-start.5 = (f32[6,20,20,6]{2,1,3,0:T(8,128)}, f32[6,20,20,6]{2,1,3,0:T(8,128)}, u32[]{:S(2)}, u32[]{:S(2)}) collective-permute-start(f32[6,20,20,6]{2,1,3,0:T(8,128)} %get-tuple-element.21), channel_id=1, source_target_pairs={{1,0},{2,1},{3,2},{4,3},{5,4},{6,5},{7,6},{8,7},{9,8},{10,9},{11,1... | collective-permute-start | bytes 172808 | tf_op jit(solution)/shard_map/ppermute | solution.py:24
  80.4 0.8 copy-start.10
  80.6 0.7 copy-start.2
  93.2 2.7 %copy-start = (f32[6,20,20,6]{3,2,1,0:T(8,128)S(1)}, f32[6,20,20,6]{3,2,1,0:T(8,128)}, u32[]{:S(2)}) copy-start(f32[6,20,20,6]{3,2,1,0:T(8,128)} %copy.40) | copy-start | bytes 172804
  102.8 1.5 %copy-start.6 = (f32[5,9,8,128]{3,2,1,0:T(8,128)S(1)}, f32[5,9,8,128]{3,2,1,0:T(8,128)}, u32[]{:S(2)}) copy-start(f32[5,9,8,128]{3,2,1,0:T(8,128)} %copy-done.5) | copy-start | bytes 552964
  102.8 1.5 %copy-start.8 = (f32[5,9,8,128]{3,2,1,0:T(8,128)S(1)}, f32[5,9,8,128]{3,2,1,0:T(8,128)}, u32[]{:S(2)}) copy-start(f32[5,9,8,128]{3,2,1,0:T(8,128)} %copy-done.7) | copy-start | bytes 552964
  102.8 1.5 %copy-start.12 = (f32[5,9,8,128]{3,2,1,0:T(8,128)S(1)}, f32[5,9,8,128]{3,2,1,0:T(8,128)}, u32[]{:S(2)}) copy-start(f32[5,9,8,128]{3,2,1,0:T(8,128)} %constant_dynamic-update-slice_fusion.4) | copy-start | bytes 552964
  102.8 1.5 %copy-start.13 = (f32[5,9,8,128]{3,2,1,0:T(8,128)S(1)}, f32[5,9,8,128]{3,2,1,0:T(8,128)}, u32[]{:S(2)}) copy-start(f32[5,9,8,128]{3,2,1,0:T(8,128)} %constant_dynamic-update-slice_fusion.9) | copy-start | bytes 552964
  102.8 1.7 %copy-start.3 = (f32[5,8,9,128]{3,2,1,0:T(8,128)S(1)}, f32[5,8,9,128]{3,2,1,0:T(8,128)}, u32[]{:S(2)}) copy-start(f32[5,8,9,128]{3,2,1,0:T(8,128)} %copy-done.2) | copy-start | bytes 552964
  102.8 1.7 %copy-start.11 = (f32[5,8,9,128]{3,2,1,0:T(8,128)S(1)}, f32[5,8,9,128]{3,2,1,0:T(8,128)}, u32[]{:S(2)}) copy-start(f32[5,8,9,128]{3,2,1,0:T(8,128)} %copy-done.10) | copy-start | bytes 552964
where the time goes:
time: 109 us
  starting transfers between devices  37.5 us (34%)
  local copies, waits for them, and re-layouts  33.5 us (31%)
  other arithmetic  27.9 us (26%)
  waiting for transfers between devices  8.86 us (8%)
  between operations  1.13 us (1%)
    ppermute x3, starting transfers between devices, extended(): lax.ppermute(head, axis, [((i + 1) % count, i) for i in range(count)])  27.6 us
    concatenate x4, other arithmetic, extended(): jnp.concatenate([lax.ppermute(tail, axis, [(i, (i + 1) % count) for i in...  14.8 us
    concatenate x2, local copies, waits for them, and re-layouts, extended(): jnp.concatenate([lax.ppermute(tail, axis, [(i, (i + 1) % count) for i in...  11.9 us
    ppermute x3, starting transfers between devices, extended(): lax.ppermute(tail, axis, [(i, (i + 1) % count) for i in range(count)])  9.9 us
    ppermute x3, local copies, waits for them, and re-layouts, extended(): lax.ppermute(head, axis, [((i + 1) % count, i) for i in range(count)])  8.7 us
    ppermute x3, local copies, waits for them, and re-layouts, extended(): lax.ppermute(tail, axis, [(i, (i + 1) % count) for i in range(count)])  7.55 us
    ppermute x3, waiting for transfers between devices, extended(): lax.ppermute(tail, axis, [(i, (i + 1) % count) for i in range(count)])  7.38 us
    div x4, other arithmetic, jacobi_sweep(): return (ALPHA * source + ALPHA * acc_num) / (centre + ALPHA * acc_den)  4.92 us
  transfers between devices with their start and end apart: 6, of which 3 were waited for; matrix products, arithmetic and copies ran while one was open for 16% of the time, Pallas kernels for 0%

commit v1 on v0

v1 whole, which is shorter than its diff:
```python
import functools

import jax
import jax.numpy as jnp
from jax import lax
from jax.experimental import pallas as pl
from jax.experimental.pallas import tpu as pltpu
from jax.sharding import PartitionSpec as P

MESH = pl.DeviceIdType.MESH
SWEEPS = 4
ALPHA = 10.0
GAMMA = 1.4
LAMBDA = 3.0
STEP_DT = 0.4

PX, PY = 2, 8
ROWS = pl.ds(PY, 8)
PLANES = pl.ds(PX, 8)


def face_state(z, a, b, c, d):
    left = [(5.0 / 6.0) * a[k] + (1.0 / 3.0) * b[k] - (1.0 / 6.0) * z[k] for k in range(5)]
    right = [(1.0 / 3.0) * a[k] + (5.0 / 6.0) * b[k] - (1.0 / 6.0) * c[k] for k in range(5)]
    rows = [None] * 5
    speeds = []
    for side, s in enumerate((left, right)):
        inv = 1.0 / s[0]
        speed = s[1 + d] * inv
        speeds.append(speed)
        kinetic = 0.5 * (s[1] * s[1] + s[2] * s[2] + s[3] * s[3]) * inv
        pressure = (GAMMA - 1.0) * (s[4] - kinetic)
        sign = 0.5 * LAMBDA if side == 0 else -0.5 * LAMBDA
        terms = [s[1 + d]]
        for k in range(3):
            t = s[1 + k] * speed
            terms.append(t + pressure if k == d else t)
        terms.append((s[4] + pressure) * speed)
        for k in range(5):
            t = 0.5 * terms[k] + sign * s[k]
            rows[k] = t if rows[k] is None else rows[k] + t
    return rows, speeds


def kernel(sizes, q_hbm, g_hbm, adv, sig, pq, zq, sg, zs, wt, src, base, spd, lsem, ssem, rsem):
    def peer(axis, step):
        n = sizes[axis]
        return {axis: lax.rem(lax.axis_index(axis) + (step + n), n)}

    faces = [("gy", 1), ("gy", -1), ("gx", 1), ("gx", -1), ("gz", 1), ("gz", -1)]
    load_q = pltpu.make_async_copy(q_hbm, pq.at[:, PLANES, ROWS, :], lsem.at[0])
    load_g = pltpu.make_async_copy(g_hbm, sg.at[0, PLANES, ROWS, :], lsem.at[1])
    load_q.start()
    load_g.start()
    barrier = pltpu.get_barrier_semaphore()
    for axis, step in faces:
        pl.semaphore_signal(barrier, inc=1, device_id=peer(axis, step), device_id_type=MESH)
    pl.semaphore_wait(barrier, 6)
    load_q.wait()
    load_g.wait()

    used = [0]
    pending = []

    def send(source, target, axis, step):
        n = used[0]
        used[0] += 1
        copy = pltpu.make_async_remote_copy(
            src_ref=source,
            dst_ref=target,
            send_sem=ssem.at[n],
            recv_sem=rsem.at[n],
            device_id=peer(axis, step),
            device_id_type=MESH,
        )
        copy.start()
        pending.append(copy)
        return copy

    def rim_copies(ref, near, far):
        w = far - near
        lead = (slice(None),) * (len(ref.shape) - 3)

        def part(planes, rows):
            return ref.at[lead + (planes, rows, slice(None))]

        out = []
        out.append(send(part(PLANES, pl.ds(PY + 8 - far, w)), part(PLANES, pl.ds(PY - far, w)), "gy", 1))
        out.append(send(part(PLANES, pl.ds(PY + near, w)), part(PLANES, pl.ds(PY + 8 + near, w)), "gy", -1))
        out.append(send(part(pl.ds(PX + 8 - far, w), ROWS), part(pl.ds(PX - far, w), ROWS), "gx", 1))
        out.append(send(part(pl.ds(PX + near, w), ROWS), part(pl.ds(PX + 8 + near, w), ROWS), "gx", -1))
        return out

    def lane_copies(source, lower, upper):
        return [send(source, lower, "gz", 1), send(source, upper, "gz", -1)]

    first = rim_copies(pq.at[pl.ds(0, 4)], 0, 1)
    first += rim_copies(sg.at[0], 0, 1)
    first += lane_copies(pq.at[pl.ds(0, 4), PLANES, ROWS, :], zq.at[0, pl.ds(0, 4)], zq.at[1, pl.ds(0, 4)])
    first += lane_copies(sg.at[0, PLANES, ROWS, :], zs.at[0, 0], zs.at[0, 1])
    second = rim_copies(pq.at[pl.ds(0, 4)], 1, 2)
    second += rim_copies(pq.at[pl.ds(4, 1)], 0, 2)
    second += lane_copies(pq.at[4, PLANES, ROWS, :], zq.at[0, 4], zq.at[1, 4])

    lane = lax.broadcasted_iota(jnp.int32, (8, 128), 1)

    def from_below(x, lower, n):
        return pltpu.roll(jnp.where(lane >= 128 - n, lower, x), n, 1)

    def from_above(x, upper, n):
        return pltpu.roll(jnp.where(lane < n, upper, x), 128 - n, 1)

    for copy in first:
        copy.wait_recv()

    def prepare(i):
        x = i + PX

        def primitive(plane, row):
            inv = 1.0 / pq[0, plane, pl.ds(row, 8), :]
            return [inv] + [pq[1 + k, plane, pl.ds(row, 8), :] * inv for k in range(3)]

        centre = primitive(x, PY)
        lo_inv = 1.0 / zq[0, 0, i]
        hi_inv = 1.0 / zq[1, 0, i]
        lo = [lo_inv] + [zq[0, 1 + k, i] * lo_inv for k in range(3)]
        hi = [hi_inv] + [zq[1, 1 + k, i] * hi_inv for k in range(3)]
        pairs = [
            (primitive(x - 1, PY), primitive(x + 1, PY)),
            (primitive(x, PY - 1), primitive(x, PY + 1)),
            ([from_below(centre[k], lo[k], 1) for k in range(4)], [from_above(centre[k], hi[k], 1) for k in range(4)]),
        ]
        grad = [[0.5 * (pairs[j][1][1 + k] - pairs[j][0][1 + k]) for j in range(3)] for k in range(3)]
        div = grad[0][0] + grad[1][1] + grad[2][2]
        source = div * div
        for k in range(3):
            source = source + grad[k][k] * grad[k][k]
        source = source + 2.0 * (grad[0][1] * grad[1][0] + grad[0][2] * grad[2][0] + grad[1][2] * grad[2][1])
        weights = [0.5 * (centre[0] + pairs[j][e][0]) for j in range(3) for e in range(2)]
        total = weights[0]
        for w in weights[1:]:
            total = total + w
        scale = ALPHA / (centre[0] + ALPHA * total)
        src[i] = source * scale
        for n in range(6):
            wt[n, i] = weights[n] * scale

    for i in range(8):
        prepare(i)

    def sweep(s):
        for i in range(8):
            x = i + PX
            here = sg[s, x, ROWS, :]
            near = [
                sg[s, x - 1, ROWS, :],
                sg[s, x + 1, ROWS, :],
                sg[s, x, pl.ds(PY - 1, 8), :],
                sg[s, x, pl.ds(PY + 1, 8), :],
                from_below(here, zs[s, 0, i], 1),
                from_above(here, zs[s, 1, i], 1),
            ]
            value = src[i]
            for n in range(6):
                value = value + wt[n, i] * near[n]
            sg[s + 1, x, ROWS, :] = value

    def sigma_copies(s, width):
        copies = rim_copies(sg.at[s], 0, width)
        return copies + lane_copies(sg.at[s, PLANES, ROWS, :], zs.at[s, 0], zs.at[s, 1])

    def stencil(fields, i, d):
        x = i + PX
        if d == 0:
            return [[pq[k, x + o, ROWS, :] for k in fields] for o in range(-2, 3)]
        if d == 1:
            return [[pq[k, x, pl.ds(PY + o, 8), :] for k in fields] for o in range(-2, 3)]
        here = [pq[k, x, ROWS, :] for k in fields]
        lo = [zq[0, k, i] for k in fields]
        hi = [zq[1, k, i] for k in fields]
        out = []
        for o in (2, 1):
            out.append([from_below(here[k], lo[k], o) for k in fields])
        out.append(here)
        for o in (1, 2):
            out.append([from_above(here[k], hi[k], o) for k in fields])
        return out

    def base_flux(d):
        def body(i, carry):
            q = stencil(range(5), i, d)
            low, low_speed = face_state(q[0], q[1], q[2], q[3], d)
            high, high_speed = face_state(q[1], q[2], q[3], q[4], d)
            for k in range(5):
                start = pq[k, i + PX, ROWS, :] if d == 0 else base[k, i]
                base[k, i] = start - STEP_DT * (high[k] - low[k])
            for n, v in enumerate(low_speed + high_speed):
                spd[4 * d + n, i] = v * (0.5 * STEP_DT)
            return carry

        lax.fori_loop(0, 8, body, 0)

    rounds = None
    for s in range(SWEEPS):
        if s:
            for copy in rounds:
                copy.wait_recv()
        sweep(s)
        rounds = sigma_copies(s + 1, 1 if s + 1 < SWEEPS else 2)
        if s == 0:
            for copy in second:
                copy.wait_recv()
        if s < 3:
            base_flux(s)
        else:
            for i in range(8):
                sig[i] = sg[SWEEPS, i + PX, ROWS, :]
    for copy in rounds:
        copy.wait_recv()

    for i in range(8):
        x = i + PX
        here = sg[SWEEPS, x, ROWS, :]
        lo, hi = zs[SWEEPS, 0, i], zs[SWEEPS, 1, i]
        lines = [
            [sg[SWEEPS, x + o, ROWS, :] for o in range(-2, 3)],
            [sg[SWEEPS, x, pl.ds(PY + o, 8), :] for o in range(-2, 3)],
            [from_below(here, lo, 2), from_below(here, lo, 1), here, from_above(here, hi, 1), from_above(here, hi, 2)],
        ]
        adv[0, i] = base[0, i]
        energy = base[4, i]
        for d in range(3):
            v = lines[d]
            left = [(5.0 / 6.0) * v[1 + e] + (1.0 / 3.0) * v[2 + e] - (1.0 / 6.0) * v[e] for e in range(2)]
            right = [(1.0 / 3.0) * v[1 + e] + (5.0 / 6.0) * v[2 + e] - (1.0 / 6.0) * v[3 + e] for e in range(2)]
            adv[1 + d, i] = base[1 + d, i] - (0.5 * STEP_DT) * ((left[1] + right[1]) - (left[0] + right[0]))
            energy = energy - (
                (left[1] * spd[4 * d + 2, i] + right[1] * spd[4 * d + 3, i])
                - (left[0] * spd[4 * d, i] + right[0] * spd[4 * d + 1, i])
            )
        adv[4, i] = energy

    for copy in pending:
        copy.wait_send()


N_COPIES = 12 + 10 + 6 * SWEEPS


def solution(mesh):
    sizes = {a: mesh.shape[a] for a in ("gx", "gy", "gz")}

    def on_device(conserved, sigma_guess):
        f32 = jnp.float32
        anywhere = pl.BlockSpec(memory_space=pl.ANY)
        vmem = pl.BlockSpec(memory_space=pltpu.VMEM)
        return pl.pallas_call(
            functools.partial(kernel, sizes),
            out_shape=(
                jax.ShapeDtypeStruct((5, 8, 8, 128), f32),
                jax.ShapeDtypeStruct((8, 8, 128), f32),
            ),
            in_specs=[anywhere, anywhere],
            out_specs=(vmem, vmem),
            scratch_shapes=[
                pltpu.VMEM((5, 12, 24, 128), f32),
                pltpu.VMEM((2, 5, 8, 8, 128), f32),
                pltpu.VMEM((SWEEPS + 1, 12, 24, 128), f32),
                pltpu.VMEM((SWEEPS + 1, 2, 8, 8, 128), f32),
                pltpu.VMEM((6, 8, 8, 128), f32),
                pltpu.VMEM((8, 8, 128), f32),
                pltpu.VMEM((5, 8, 8, 128), f32),
                pltpu.VMEM((12, 8, 8, 128), f32),
                pltpu.SemaphoreType.DMA((2,)),
                pltpu.SemaphoreType.DMA((N_COPIES,)),
                pltpu.SemaphoreType.DMA((N_COPIES,)),
            ],
            compiler_params=pltpu.CompilerParams(collective_id=0, has_side_effects=True),
        )(conserved, sigma_guess)

    return jax.shard_map(
        on_device,
        mesh=mesh,
        in_specs=(P(None, "gx", "gy", "gz"), P("gx", "gy", "gz")),
        out_specs=(P(None, "gx", "gy", "gz"), P("gx", "gy", "gz")),
        check_vma=False,
    )
```

time: 109 us -> 44.8 us (0.41)
  the two profiles are of different devices: /device:TPU:32 before, /device:TPU:1 now
where the time goes in v1:
time: 44.8 us; the launch traced here: 44.7 us
  Pallas kernels  41.8 us (93%)
  local copies, waits for them, and re-layouts  2.22 us (5%)
  between operations  0.65 us (1%)
    pallas_call x1, Pallas kernels, on_device(): pl.pallas_call(functools.partial(kernel, sizes), out_shape=(jax.ShapeDtyp...  41.8 us
    unnamed x4, local copies, waits for them, and re-layouts  2.22 us

profile of v1, /device:TPU:1, one launch (start us, length us, event | category | flops | bytes accessed | tf_op | source)
XLA Modules:
  0.0 44.7 jit_solution(9370477857913274658)
XLA Ops:
  0.6 41.8 %shard_map.41 = (f32[5,8,8,128]{3,2,1,0:T(8,128)}, f32[8,8,128]{2,1,0:T(8,128)}) custom-call(f32[5,8,8,128]{3,2,1,0:T(8,128)} %q_hbm.1, f32[8,8,128]{2,1,0:T(8,128)} %g_hbm.1), custom_call_target="tpu_custom_call" | custom-call | tf_op jit(solution)/shard_map/pallas_call | solution.py:257
  42.5 0.0 copy-start
  42.5 1.6 %copy.6 = f32[5,8,8,128]{3,2,1,0:T(8,128)} copy(f32[5,8,8,128]{3,2,1,0:T(8,128)} %get-tuple-element.4) | data formatting | bytes 327680
  44.1 0.0 copy-done
  44.1 0.6 %copy.7 = f32[8,8,128]{2,1,0:T(8,128)} copy(f32[8,8,128]{2,1,0:T(8,128)S(1)} %copy-done) | data formatting | bytes 65536
Async XLA Ops:
  42.5 1.6 %copy-start = (f32[8,8,128]{2,1,0:T(8,128)S(1)}, f32[8,8,128]{2,1,0:T(8,128)}, u32[]{:S(2)}) copy-start(f32[8,8,128]{2,1,0:T(8,128)} %get-tuple-element.5) | copy-start | bytes 98308

commit v2 on v1

v2 whole, which is shorter than its diff:
```python
import functools

import jax
import jax.numpy as jnp
from jax import lax
from jax.experimental import pallas as pl
from jax.experimental.pallas import tpu as pltpu
from jax.sharding import PartitionSpec as P

MESH = pl.DeviceIdType.MESH
SWEEPS = 4
ALPHA = 10.0
GAMMA = 1.4
LAMBDA = 3.0
STEP_DT = 0.4

PX, PY = 3, 8
N_X, N_Y = 14, 24
ROWS = pl.ds(PY, 8)
PLANES = pl.ds(PX, 8)
FACES = [(0, 1, 0), (0, -1, 0), (1, 0, 0), (-1, 0, 0), (0, 0, 1), (0, 0, -1)]
EDGES = [(i, j, k) for i in (1, -1, 0) for j in (1, -1, 0) for k in (1, -1, 0) if abs(i) + abs(j) + abs(k) == 2]


def face_state(z, a, b, c, d):
    left = [(5.0 / 6.0) * a[k] + (1.0 / 3.0) * b[k] - (1.0 / 6.0) * z[k] for k in range(5)]
    right = [(1.0 / 3.0) * a[k] + (5.0 / 6.0) * b[k] - (1.0 / 6.0) * c[k] for k in range(5)]
    rows = [None] * 5
    speeds = []
    for side, s in enumerate((left, right)):
        inv = 1.0 / s[0]
        speed = s[1 + d] * inv
        speeds.append(speed)
        kinetic = 0.5 * (s[1] * s[1] + s[2] * s[2] + s[3] * s[3]) * inv
        pressure = (GAMMA - 1.0) * (s[4] - kinetic)
        sign = 0.5 * LAMBDA if side == 0 else -0.5 * LAMBDA
        terms = [s[1 + d]]
        for k in range(3):
            t = s[1 + k] * speed
            terms.append(t + pressure if k == d else t)
        terms.append((s[4] + pressure) * speed)
        for k in range(5):
            t = 0.5 * terms[k] + sign * s[k]
            rows[k] = t if rows[k] is None else rows[k] + t
    return rows, speeds


def kernel(
    sizes, q_hbm, g_hbm, adv, sig, pq, zq, sg, zs, src, zsrc, wt, sw, wb, sb, base, spd, lsem, ssem, rsem
):
    def peer(offset):
        out = {}
        for axis, step in zip(("gx", "gy", "gz"), offset):
            if step:
                n = sizes[axis]
                out[axis] = lax.rem(lax.axis_index(axis) + (step + n), n)
        return out

    load_q = pltpu.make_async_copy(q_hbm, pq.at[:, PLANES, ROWS, :], lsem.at[0])
    load_g = pltpu.make_async_copy(g_hbm, sg.at[0, PLANES, ROWS, :], lsem.at[1])
    load_q.start()
    load_g.start()
    barrier = pltpu.get_barrier_semaphore()
    for offset in FACES:
        pl.semaphore_signal(barrier, inc=1, device_id=peer(offset), device_id_type=MESH)
    pl.semaphore_wait(barrier, 6)
    load_q.wait()
    load_g.wait()

    pending = []

    def send(source, target, offset):
        n = len(pending)
        copy = pltpu.make_async_remote_copy(
            src_ref=source,
            dst_ref=target,
            send_sem=ssem.at[n],
            recv_sem=rsem.at[n],
            device_id=peer(offset),
            device_id_type=MESH,
        )
        copy.start()
        pending.append(copy)
        return copy

    def span(step, start, near, far):
        w = far - near
        if step == 0:
            return pl.ds(start, 8), pl.ds(start, 8)
        if step > 0:
            return pl.ds(start + 8 - far, w), pl.ds(start - far, w)
        return pl.ds(start + near, w), pl.ds(start + 8 + near, w)

    def share(offset, centre, lower, upper, near, far, near_y=None, far_y=None):
        planes, planes_to = span(offset[0], PX, near, far)
        rows, rows_to = span(offset[1], PY, near if near_y is None else near_y, far if far_y is None else far_y)
        lead = (slice(None),) * (len(centre.shape) - 3)
        target = {0: centre, 1: lower, -1: upper}[offset[2]]
        return send(
            centre.at[lead + (planes, rows, slice(None))],
            target.at[lead + (planes_to, rows_to, slice(None))],
            offset,
        )

    def sigma(s):
        return sg.at[s], zs.at[s, 0], zs.at[s, 1]

    def fields(a, n):
        k = pl.ds(a, n)
        return pq.at[k], zq.at[0, k], zq.at[1, k]

    first = [share(o, *fields(0, 4), 0, 1) for o in FACES]
    first += [share(o, *sigma(0), 0, 1) for o in FACES]
    second = [share(o, *fields(0, 4), 1, 2) for o in FACES[:4]]
    second += [share(o, *fields(4, 1), 0, 2) for o in FACES]

    lane = lax.broadcasted_iota(jnp.int32, (8, 128), 1)

    def from_below(x, lower, n):
        return pltpu.roll(jnp.where(lane >= 128 - n, lower, x), n, 1)

    def from_above(x, upper, n):
        return pltpu.roll(jnp.where(lane < n, upper, x), 128 - n, 1)

    def strip(lower, here, upper):
        outer = jnp.where(lane >= 64, lower, here)
        inner = jnp.where(lane >= 64, here, upper)
        return jnp.where((lane >= 32) & (lane < 96), pltpu.roll(inner, 64, 1), outer)

    for copy in first:
        copy.wait_recv()
    corner = [share(o, *fields(0, 1), 0, 1) for o in EDGES]

    def scaled(centre, around):
        weights = [0.5 * (centre + n) for n in around]
        total = weights[0]
        for w in weights[1:]:
            total = total + w
        scale = ALPHA / (centre + ALPHA * total)
        return scale, [w * scale for w in weights]

    def prepare(i):
        x = i + PX

        def primitive(plane, row):
            inv = 1.0 / pq[0, plane, pl.ds(row, 8), :]
            return [inv] + [pq[1 + k, plane, pl.ds(row, 8), :] * inv for k in range(3)]

        def beyond(side):
            inv = 1.0 / zq[side, 0, x, ROWS, :]
            return [inv] + [zq[side, 1 + k, x, ROWS, :] * inv for k in range(3)]

        centre = primitive(x, PY)
        lo, hi = beyond(0), beyond(1)
        pairs = [
            (primitive(x - 1, PY), primitive(x + 1, PY)),
            (primitive(x, PY - 1), primitive(x, PY + 1)),
            ([from_below(centre[k], lo[k], 1) for k in range(4)], [from_above(centre[k], hi[k], 1) for k in range(4)]),
        ]
        grad = [[0.5 * (pairs[j][1][1 + k] - pairs[j][0][1 + k]) for j in range(3)] for k in range(3)]
        div = grad[0][0] + grad[1][1] + grad[2][2]
        source = div * div
        for k in range(3):
            source = source + grad[k][k] * grad[k][k]
        source = source + 2.0 * (grad[0][1] * grad[1][0] + grad[0][2] * grad[2][0] + grad[1][2] * grad[2][1])
        scale, weights = scaled(centre[0], [pairs[j][e][0] for j in range(3) for e in range(2)])
        src[x, ROWS, :] = source
        sw[x, ROWS, :] = source * scale
        for n in range(6):
            wt[n, x, ROWS, :] = weights[n]

    for i in range(8):
        prepare(i)
    sources = (src, zsrc.at[0], zsrc.at[1])
    outer = [share(o, *sources, 0, 1) for o in FACES]

    def relax(s, x, row):
        r = pl.ds(row, 8)
        here = sg[s, x, r, :]
        near = [
            sg[s, x - 1, r, :],
            sg[s, x + 1, r, :],
            sg[s, x, pl.ds(row - 1, 8), :],
            sg[s, x, pl.ds(row + 1, 8), :],
            from_below(here, zs[s, 0, x, r, :], 1),
            from_above(here, zs[s, 1, x, r, :], 1),
        ]
        value = sw[x, r, :]
        for n in range(6):
            value = value + wt[n, x, r, :] * near[n]
        sg[s + 1, x, r, :] = value

    def strip_of(centre, lower, upper):
        return lambda x, row: strip(*[v[x, pl.ds(row, 8), :] for v in (lower, centre, upper)])

    def relax_strips(s):
        at = strip_of(*sigma(s))
        level = [at(x, PY) for x in range(PX - 1, PX + 9)]
        for i in range(8):
            x = i + PX
            here = level[i + 1]
            near = [
                level[i],
                level[i + 2],
                at(x, PY - 1),
                at(x, PY + 1),
                pltpu.roll(here, 1, 1),
                pltpu.roll(here, 127, 1),
            ]
            value = sb[i]
            for n in range(6):
                value = value + wb[n, i] * near[n]
            zs[s + 1, 0, x, ROWS, :] = value
            zs[s + 1, 1, x, ROWS, :] = pltpu.roll(value, 64, 1)

    def relax_wide(s, depth):
        for x in [*range(PX - depth, PX), *range(PX + 8, PX + 8 + depth)]:
            relax(s, x, PY)
        for x in range(PX, PX + 8):
            relax(s, x, PY - depth)
            relax(s, x, PY + depth)
        relax_strips(s)

    def widen_tile(x, row):
        r = pl.ds(row, 8)
        centre = 1.0 / pq[0, x, r, :]
        scale, weights = scaled(
            centre,
            [
                1.0 / pq[0, x - 1, r, :],
                1.0 / pq[0, x + 1, r, :],
                1.0 / pq[0, x, pl.ds(row - 1, 8), :],
                1.0 / pq[0, x, pl.ds(row + 1, 8), :],
                from_below(centre, 1.0 / zq[0, 0, x, r, :], 1),
                from_above(centre, 1.0 / zq[1, 0, x, r, :], 1),
            ],
        )
        sw[x, r, :] = src[x, r, :] * scale
        for n in range(6):
            wt[n, x, r, :] = weights[n]

    def widen(depth):
        for x in [*range(PX - depth, PX), *range(PX + 8, PX + 8 + depth)]:
            widen_tile(x, PY)
        density = strip_of(pq.at[0], zq.at[0, 0], zq.at[1, 0])
        source = strip_of(src, zsrc.at[0], zsrc.at[1])

        def body(i, carry):
            x = i + PX
            widen_tile(x, PY - depth)
            widen_tile(x, PY + depth)
            if depth > 1:
                return carry
            centre = 1.0 / density(x, PY)
            scale, weights = scaled(
                centre,
                [
                    1.0 / density(x - 1, PY),
                    1.0 / density(x + 1, PY),
                    1.0 / density(x, PY - 1),
                    1.0 / density(x, PY + 1),
                    pltpu.roll(centre, 1, 1),
                    pltpu.roll(centre, 127, 1),
                ],
            )
            sb[i] = source(x, PY) * scale
            for n in range(6):
                wb[n, i] = weights[n]
            return carry

        lax.fori_loop(0, 8, body, 0)

    def stencil(i, d):
        x = i + PX
        if d == 0:
            return [[pq[k, x + o, ROWS, :] for k in range(5)] for o in range(-2, 3)]
        if d == 1:
            return [[pq[k, x, pl.ds(PY + o, 8), :] for k in range(5)] for o in range(-2, 3)]
        here = [pq[k, x, ROWS, :] for k in range(5)]
        lo = [zq[0, k, x, ROWS, :] for k in range(5)]
        hi = [zq[1, k, x, ROWS, :] for k in range(5)]
        out = [[from_below(here[k], lo[k], o) for k in range(5)] for o in (2, 1)]
        out.append(here)
        out += [[from_above(here[k], hi[k], o) for k in range(5)] for o in (1, 2)]
        return out

    def base_flux(d):
        def body(i, carry):
            q = stencil(i, d)
            low, low_speed = face_state(q[0], q[1], q[2], q[3], d)
            high, high_speed = face_state(q[1], q[2], q[3], q[4], d)
            for k in range(5):
                start = pq[k, i + PX, ROWS, :] if d == 0 else base[k, i]
                base[k, i] = start - STEP_DT * (high[k] - low[k])
            for n, v in enumerate(low_speed + high_speed):
                spd[4 * d + n, i] = v * (0.5 * STEP_DT)
            return carry

        lax.fori_loop(0, 8, body, 0)

    for x in range(PX, PX + 8):
        relax(0, x, PY)
    rounds = [share(o, *sigma(1), 0, 1) for o in EDGES]
    rounds += [share(o, *sigma(1), 0, 2) for o in FACES]
    late = [share(o, *sources, 1, 2) for o in FACES[:4]]
    late += [share(o, *fields(0, 1), 2, 3) for o in FACES[:4]]
    for o in EDGES:
        if o[2]:
            late.append(share(o, *fields(0, 1), 1, 2))
        else:
            late.append(share(o, *fields(0, 1), 1, 2, 0, 1))
            late.append(share(o, *fields(0, 1), 0, 1, 1, 2))

    for copy in second:
        copy.wait_recv()
    base_flux(0)
    base_flux(1)
    for copy in corner + outer:
        copy.wait_recv()
    widen(1)
    for copy in rounds:
        copy.wait_recv()
    relax_wide(1, 1)
    for x in range(PX, PX + 8):
        relax(2, x, PY)
    rounds = [share(o, *sigma(3), 0, 2) for o in EDGES] + [share(o, *sigma(3), 0, 3) for o in FACES]
    base_flux(2)
    for copy in late:
        copy.wait_recv()
    widen(2)
    for copy in rounds:
        copy.wait_recv()
    relax_wide(3, 2)

    for i in range(8):
        x = i + PX
        here = sg[SWEEPS, x, ROWS, :]
        sig[i] = here
        lo, hi = zs[SWEEPS, 0, x, ROWS, :], zs[SWEEPS, 1, x, ROWS, :]
        lines = [
            [sg[SWEEPS, x + o, ROWS, :] for o in range(-2, 3)],
            [sg[SWEEPS, x, pl.ds(PY + o, 8), :] for o in range(-2, 3)],
            [from_below(here, lo, 2), from_below(here, lo, 1), here, from_above(here, hi, 1), from_above(here, hi, 2)],
        ]
        adv[0, i] = base[0, i]
        energy = base[4, i]
        for d in range(3):
            v = lines[d]
            left = [(5.0 / 6.0) * v[1 + e] + (1.0 / 3.0) * v[2 + e] - (1.0 / 6.0) * v[e] for e in range(2)]
            right = [(1.0 / 3.0) * v[1 + e] + (5.0 / 6.0) * v[2 + e] - (1.0 / 6.0) * v[3 + e] for e in range(2)]
            adv[1 + d, i] = base[1 + d, i] - (0.5 * STEP_DT) * ((left[1] + right[1]) - (left[0] + right[0]))
            energy = energy - (
                (left[1] * spd[4 * d + 2, i] + right[1] * spd[4 * d + 3, i])
                - (left[0] * spd[4 * d, i] + right[0] * spd[4 * d + 1, i])
            )
        adv[4, i] = energy

    for copy in pending:
        copy.wait_send()


def write_out(adv, sig, adv_out, sig_out, sem):
    a = pltpu.make_async_copy(adv, adv_out, sem.at[0])
    b = pltpu.make_async_copy(sig, sig_out, sem.at[1])
    a.start()
    b.start()
    a.wait()
    b.wait()


N_COPIES = 100


def solution(mesh):
    sizes = {a: mesh.shape[a] for a in ("gx", "gy", "gz")}

    def on_device(conserved, sigma_guess):
        f32 = jnp.float32
        anywhere = pl.BlockSpec(memory_space=pl.ANY)
        vmem = pl.BlockSpec(memory_space=pltpu.VMEM)
        shapes = (
            jax.ShapeDtypeStruct((5, 8, 8, 128), f32),
            jax.ShapeDtypeStruct((8, 8, 128), f32),
        )
        made = pl.pallas_call(
            functools.partial(kernel, sizes),
            out_shape=shapes,
            in_specs=[anywhere, anywhere],
            out_specs=(vmem, vmem),
            scratch_shapes=[
                pltpu.VMEM((5, N_X, N_Y, 128), f32),
                pltpu.VMEM((2, 5, N_X, N_Y, 128), f32),
                pltpu.VMEM((SWEEPS + 1, N_X, N_Y, 128), f32),
                pltpu.VMEM((SWEEPS + 1, 2, N_X, N_Y, 128), f32),
                pltpu.VMEM((N_X, N_Y, 128), f32),
                pltpu.VMEM((2, N_X, N_Y, 128), f32),
                pltpu.VMEM((6, N_X, N_Y, 128), f32),
                pltpu.VMEM((N_X, N_Y, 128), f32),
                pltpu.VMEM((6, 8, 8, 128), f32),
                pltpu.VMEM((8, 8, 128), f32),
                pltpu.VMEM((5, 8, 8, 128), f32),
                pltpu.VMEM((12, 8, 8, 128), f32),
                pltpu.SemaphoreType.DMA((2,)),
                pltpu.SemaphoreType.DMA((N_COPIES,)),
                pltpu.SemaphoreType.DMA((N_COPIES,)),
            ],
            compiler_params=pltpu.CompilerParams(collective_id=0, has_side_effects=True, vmem_limit_bytes=16777216),
        )(*[pltpu.with_memory_space_constraint(v, pltpu.HBM) for v in (conserved, sigma_guess)])
        return pl.pallas_call(
            write_out,
            out_shape=shapes,
            in_specs=[vmem, vmem],
            out_specs=(anywhere, anywhere),
            scratch_shapes=[pltpu.SemaphoreType.DMA((2,))],
            compiler_params=pltpu.CompilerParams(vmem_limit_bytes=16777216),
        )(*made)

    return jax.shard_map(
        on_device,
        mesh=mesh,
        in_specs=(P(None, "gx", "gy", "gz"), P("gx", "gy", "gz")),
        out_specs=(P(None, "gx", "gy", "gz"), P("gx", "gy", "gz")),
        check_vma=False,
    )
```

time: 44.8 us -> 40.6 us (0.906)
  local copies, waits for them, and re-layouts: 2.22 us -> 0 us
  Pallas kernels: 41.8 us -> 39.8 us
    unnamed x4 -> x0, local copies, waits for them, and re-layouts: 2.22 us -> none
    pallas_call x1 -> x2, Pallas kernels: 41.8 us -> 39.8 us  [the longest x1 39.1 us: on_device(): pl.pallas_call(functools.partial(kernel, sizes), out_shape=shapes, in_spe...]
where the time goes in v2:
time: 40.6 us; the launch traced here: 40.4 us
  Pallas kernels  39.8 us (98%)
  between operations  0.64 us (2%)
    pallas_call x1, Pallas kernels, on_device(): pl.pallas_call(functools.partial(kernel, sizes), out_shape=shapes, in_spe...  39.1 us

profile of v2, /device:TPU:1, one launch (start us, length us, event | category | flops | bytes accessed | tf_op | source)
XLA Modules:
  0.0 40.4 jit_solution(11894807254769551742)
XLA Ops:
  0.6 39.1 %shard_map.41 = (f32[5,8,8,128]{3,2,1,0:T(8,128)S(1)}, f32[8,8,128]{2,1,0:T(8,128)S(1)}) custom-call(f32[5,8,8,128]{3,2,1,0:T(8,128)} %q_hbm.1, f32[8,8,128]{2,1,0:T(8,128)} %g_hbm.1), custom_call_target="tpu_custom_call" | custom-call | tf_op jit(solution)/shard_map/pallas_call | solution.py:385
  39.7 0.7 %shard_map.42 = (f32[5,8,8,128]{3,2,1,0:T(8,128)}, f32[8,8,128]{2,1,0:T(8,128)}) custom-call(f32[5,8,8,128]{3,2,1,0:T(8,128)S(1)} %get-tuple-element.4.adv, f32[8,8,128]{2,1,0:T(8,128)S(1)} %get-tuple-element.5.sig), custom_call_target="tpu_custom_call" | custom-call | tf_op jit(solution)/shard_map/pallas_call | solution.py:409

commit v3 on v2

--- a/solution.py
+++ b/solution.py
@@ -19,6 +19,8 @@
 ROWS = pl.ds(PY, 8)
 PLANES = pl.ds(PX, 8)
 FACES = [(0, 1, 0), (0, -1, 0), (1, 0, 0), (-1, 0, 0), (0, 0, 1), (0, 0, -1)]
+FIRST, DENSITY, ENERGY, SOURCE, SIGMA_1, LATE, SECOND, SIGMA_3 = range(8)
+N_GROUPS = 8
 EDGES = [(i, j, k) for i in (1, -1, 0) for j in (1, -1, 0) for k in (1, -1, 0) if abs(i) + abs(j) + abs(k) == 2]
 
 
@@ -46,7 +48,7 @@
 
 
 def kernel(
-    sizes, q_hbm, g_hbm, adv, sig, pq, zq, sg, zs, src, zsrc, wt, sw, wb, sb, base, spd, lsem, ssem, rsem
+    sizes, q_hbm, g_hbm, adv, sig, pq, zq, sg, zs, src, zsrc, wt, sw, wb, sb, base, spd, rows_ref, lsem, ssem, rsem
 ):
     def peer(offset):
         out = {}
@@ -67,21 +69,36 @@
     load_q.wait()
     load_g.wait()
 
-    pending = []
-
-    def send(source, target, offset):
-        n = len(pending)
-        copy = pltpu.make_async_remote_copy(
+    sent = [0] * N_GROUPS
+
+    def send(source, target, offset, group):
+        rows = 1
+        for n in source.shape[:-1]:
+            rows *= n
+        sent[group] += rows
+        pltpu.make_async_remote_copy(
             src_ref=source,
             dst_ref=target,
-            send_sem=ssem.at[n],
-            recv_sem=rsem.at[n],
+            send_sem=ssem.at[0],
+            recv_sem=rsem.at[group],
             device_id=peer(offset),
             device_id_type=MESH,
+        ).start()
+
+    def all_rows(rows, group):
+        span_ref = rows_ref.at[pl.ds(0, rows)]
+        return pltpu.make_async_remote_copy(
+            src_ref=span_ref,
+            dst_ref=span_ref,
+            send_sem=ssem.at[0],
+            recv_sem=rsem.at[group],
+            device_id=peer(FACES[0]),
+            device_id_type=MESH,
         )
-        copy.start()
-        pending.append(copy)
-        return copy
+
+    def arrived(*groups):
+        for group in groups:
+            all_rows(sent[group], group).wait_recv()
 
     def span(step, start, near, far):
         w = far - near
@@ -91,15 +108,16 @@
             return pl.ds(start + 8 - far, w), pl.ds(start - far, w)
         return pl.ds(start + near, w), pl.ds(start + 8 + near, w)
 
-    def share(offset, centre, lower, upper, near, far, near_y=None, far_y=None):
+    def share(group, offset, centre, lower, upper, near, far, near_y=None, far_y=None):
         planes, planes_to = span(offset[0], PX, near, far)
         rows, rows_to = span(offset[1], PY, near if near_y is None else near_y, far if far_y is None else far_y)
         lead = (slice(None),) * (len(centre.shape) - 3)
         target = {0: centre, 1: lower, -1: upper}[offset[2]]
-        return send(
+        send(
             centre.at[lead + (planes, rows, slice(None))],
             target.at[lead + (planes_to, rows_to, slice(None))],
             offset,
+            group,
         )
 
     def sigma(s):
@@ -109,10 +127,9 @@
         k = pl.ds(a, n)
         return pq.at[k], zq.at[0, k], zq.at[1, k]
 
-    first = [share(o, *fields(0, 4), 0, 1) for o in FACES]
-    first += [share(o, *sigma(0), 0, 1) for o in FACES]
-    second = [share(o, *fields(0, 4), 1, 2) for o in FACES[:4]]
-    second += [share(o, *fields(4, 1), 0, 2) for o in FACES]
+    for o in FACES:
+        share(FIRST, o, *fields(0, 4), 0, 1)
+        share(FIRST, o, *sigma(0), 0, 1)
 
     lane = lax.broadcasted_iota(jnp.int32, (8, 128), 1)
 
@@ -127,9 +144,13 @@
         inner = jnp.where(lane >= 64, here, upper)
         return jnp.where((lane >= 32) & (lane < 96), pltpu.roll(inner, 64, 1), outer)
 
-    for copy in first:
-        copy.wait_recv()
-    corner = [share(o, *fields(0, 1), 0, 1) for o in EDGES]
+    arrived(FIRST)
+    for o in EDGES:
+        share(DENSITY, o, *fields(0, 1), 0, 1)
+    for o in FACES[:4]:
+        share(DENSITY, o, *fields(0, 1), 1, 2)
+    for o in FACES[4:]:
+        share(ENERGY, o, *fields(4, 1), 0, 2)
 
     def scaled(centre, around):
         weights = [0.5 * (centre + n) for n in around]
@@ -168,11 +189,6 @@
         sw[x, ROWS, :] = source * scale
         for n in range(6):
             wt[n, x, ROWS, :] = weights[n]
-
-    for i in range(8):
-        prepare(i)
-    sources = (src, zsrc.at[0], zsrc.at[1])
-    outer = [share(o, *sources, 0, 1) for o in FACES]
 
     def relax(s, x, row):
         r = pl.ds(row, 8)
@@ -245,12 +261,12 @@
         density = strip_of(pq.at[0], zq.at[0, 0], zq.at[1, 0])
         source = strip_of(src, zsrc.at[0], zsrc.at[1])
 
-        def body(i, carry):
+        for i in range(8):
             x = i + PX
             widen_tile(x, PY - depth)
             widen_tile(x, PY + depth)
             if depth > 1:
-                return carry
+                continue
             centre = 1.0 / density(x, PY)
             scale, weights = scaled(
                 centre,
@@ -266,9 +282,6 @@
             sb[i] = source(x, PY) * scale
             for n in range(6):
                 wb[n, i] = weights[n]
-            return carry
-
-        lax.fori_loop(0, 8, body, 0)
 
     def stencil(i, d):
         x = i + PX
@@ -290,7 +303,7 @@
             low, low_speed = face_state(q[0], q[1], q[2], q[3], d)
             high, high_speed = face_state(q[1], q[2], q[3], q[4], d)
             for k in range(5):
-                start = pq[k, i + PX, ROWS, :] if d == 0 else base[k, i]
+                start = pq[k, i + PX, ROWS, :] if d == 2 else base[k, i]
                 base[k, i] = start - STEP_DT * (high[k] - low[k])
             for n, v in enumerate(low_speed + high_speed):
                 spd[4 * d + n, i] = v * (0.5 * STEP_DT)
@@ -298,38 +311,56 @@
 
         lax.fori_loop(0, 8, body, 0)
 
-    for x in range(PX, PX + 8):
-        relax(0, x, PY)
-    rounds = [share(o, *sigma(1), 0, 1) for o in EDGES]
-    rounds += [share(o, *sigma(1), 0, 2) for o in FACES]
-    late = [share(o, *sources, 1, 2) for o in FACES[:4]]
-    late += [share(o, *fields(0, 1), 2, 3) for o in FACES[:4]]
+    sources = (src, zsrc.at[0], zsrc.at[1])
+    far_edges = [o for o in EDGES if o[0]]
+    near_edges = [o for o in EDGES if not o[0]]
+    for planes, edges, faces in (((0, 7, 1, 6), far_edges, FACES[2:4]), ((2, 5, 3, 4), near_edges, FACES[:2] + FACES[4:])):
+        for i in planes:
+            prepare(i)
+        for i in planes:
+            relax(0, i + PX, PY)
+        for o in edges:
+            share(SIGMA_1, o, *sigma(1), 0, 1)
+        for o in faces:
+            share(SOURCE, o, *sources, 0, 1)
+            share(SIGMA_1, o, *sigma(1), 0, 2)
+    for o in FACES[:4]:
+        share(LATE, o, *sources, 1, 2)
+        share(LATE, o, *fields(0, 1), 2, 3)
     for o in EDGES:
         if o[2]:
-            late.append(share(o, *fields(0, 1), 1, 2))
+            share(LATE, o, *fields(0, 1), 1, 2)
         else:
-            late.append(share(o, *fields(0, 1), 1, 2, 0, 1))
-            late.append(share(o, *fields(0, 1), 0, 1, 1, 2))
-
-    for copy in second:
-        copy.wait_recv()
+            share(LATE, o, *fields(0, 1), 1, 2, 0, 1)
+            share(LATE, o, *fields(0, 1), 0, 1, 1, 2)
+    for o in FACES[:4]:
+        share(SECOND, o, *fields(1, 3), 1, 2)
+        share(SECOND, o, *fields(4, 1), 0, 2)
+
+    arrived(ENERGY)
+    base_flux(2)
+    arrived(DENSITY, SOURCE)
+    widen(1)
+    arrived(SIGMA_1)
+    relax_wide(1, 1)
+    for i in (0, 7, 1, 6, 2, 5):
+        relax(2, i + PX, PY)
+    for o in far_edges:
+        share(SIGMA_3, o, *sigma(3), 0, 2)
+    for o in FACES[2:4]:
+        share(SIGMA_3, o, *sigma(3), 0, 3)
+    for i in (3, 4):
+        relax(2, i + PX, PY)
+    for o in near_edges:
+        share(SIGMA_3, o, *sigma(3), 0, 2)
+    for o in FACES[:2] + FACES[4:]:
+        share(SIGMA_3, o, *sigma(3), 0, 3)
+    arrived(LATE)
+    widen(2)
+    arrived(SECOND)
     base_flux(0)
     base_flux(1)
-    for copy in corner + outer:
-        copy.wait_recv()
-    widen(1)
-    for copy in rounds:
-        copy.wait_recv()
-    relax_wide(1, 1)
-    for x in range(PX, PX + 8):
-        relax(2, x, PY)
-    rounds = [share(o, *sigma(3), 0, 2) for o in EDGES] + [share(o, *sigma(3), 0, 3) for o in FACES]
-    base_flux(2)
-    for copy in late:
-        copy.wait_recv()
-    widen(2)
-    for copy in rounds:
-        copy.wait_recv()
+    arrived(SIGMA_3)
     relax_wide(3, 2)
 
     for i in range(8):
@@ -343,20 +374,19 @@
             [from_below(here, lo, 2), from_below(here, lo, 1), here, from_above(here, hi, 1), from_above(here, hi, 2)],
         ]
         adv[0, i] = base[0, i]
-        energy = base[4, i]
+        total = base[4, i]
         for d in range(3):
             v = lines[d]
             left = [(5.0 / 6.0) * v[1 + e] + (1.0 / 3.0) * v[2 + e] - (1.0 / 6.0) * v[e] for e in range(2)]
             right = [(1.0 / 3.0) * v[1 + e] + (5.0 / 6.0) * v[2 + e] - (1.0 / 6.0) * v[3 + e] for e in range(2)]
             adv[1 + d, i] = base[1 + d, i] - (0.5 * STEP_DT) * ((left[1] + right[1]) - (left[0] + right[0]))
-            energy = energy - (
+            total = total - (
                 (left[1] * spd[4 * d + 2, i] + right[1] * spd[4 * d + 3, i])
                 - (left[0] * spd[4 * d, i] + right[0] * spd[4 * d + 1, i])
             )
-        adv[4, i] = energy
-
-    for copy in pending:
-        copy.wait_send()
+        adv[4, i] = total
+
+    all_rows(sum(sent), FIRST).wait_send()
 
 
 def write_out(adv, sig, adv_out, sig_out, sem):
@@ -366,9 +396,6 @@
     b.start()
     a.wait()
     b.wait()
-
-
-N_COPIES = 100
 
 
 def solution(mesh):
@@ -400,9 +427,10 @@
                 pltpu.VMEM((8, 8, 128), f32),
                 pltpu.VMEM((5, 8, 8, 128), f32),
                 pltpu.VMEM((12, 8, 8, 128), f32),
+                pltpu.VMEM((4096, 128), f32),
                 pltpu.SemaphoreType.DMA((2,)),
-                pltpu.SemaphoreType.DMA((N_COPIES,)),
-                pltpu.SemaphoreType.DMA((N_COPIES,)),
+                pltpu.SemaphoreType.DMA((1,)),
+                pltpu.SemaphoreType.DMA((N_GROUPS,)),
             ],
             compiler_params=pltpu.CompilerParams(collective_id=0, has_side_effects=True, vmem_limit_bytes=16777216),
         )(*[pltpu.with_memory_space_constraint(v, pltpu.HBM) for v in (conserved, sigma_guess)])

time: 40.6 us -> 38.8 us (0.956)
  Pallas kernels: 39.8 us -> 37.9 us
    pallas_call x1, Pallas kernels: 39.1 us -> 37.2 us  [on_device(): pl.pallas_call(functools.partial(kernel, sizes), out_shape=shapes, in_spe...]
where the time goes in v3:
time: 38.8 us; the launch traced here: 38.6 us
  Pallas kernels  37.9 us (98%)
  between operations  0.64 us (2%)
    pallas_call x1, Pallas kernels, on_device(): pl.pallas_call(functools.partial(kernel, sizes), out_shape=shapes, in_spe...  37.2 us

profile of v3, /device:TPU:1, one launch (start us, length us, event | category | flops | bytes accessed | tf_op | source)
XLA Modules:
  0.0 38.6 jit_solution(14035532582648028838)
XLA Ops:
  0.6 37.2 %shard_map.41 = (f32[5,8,8,128]{3,2,1,0:T(8,128)S(1)}, f32[8,8,128]{2,1,0:T(8,128)S(1)}) custom-call(f32[5,8,8,128]{3,2,1,0:T(8,128)} %q_hbm.1, f32[8,8,128]{2,1,0:T(8,128)} %g_hbm.1), custom_call_target="tpu_custom_call" | custom-call | tf_op jit(solution)/shard_map/pallas_call | solution.py:412
  37.9 0.7 %shard_map.42 = (f32[5,8,8,128]{3,2,1,0:T(8,128)}, f32[8,8,128]{2,1,0:T(8,128)}) custom-call(f32[5,8,8,128]{3,2,1,0:T(8,128)S(1)} %get-tuple-element.4.adv, f32[8,8,128]{2,1,0:T(8,128)S(1)} %get-tuple-element.5.sig), custom_call_target="tpu_custom_call" | custom-call | tf_op jit(solution)/shard_map/pallas_call | solution.py:437

commit v4 on v3

--- a/solution.py
+++ b/solution.py
@@ -19,9 +19,11 @@
 ROWS = pl.ds(PY, 8)
 PLANES = pl.ds(PX, 8)
 FACES = [(0, 1, 0), (0, -1, 0), (1, 0, 0), (-1, 0, 0), (0, 0, 1), (0, 0, -1)]
+EDGES = [(i, j, k) for i in (1, -1, 0) for j in (1, -1, 0) for k in (1, -1, 0) if abs(i) + abs(j) + abs(k) == 2]
+BESIDE = [o for o in EDGES if o[2]]
+DIAGONAL = [o for o in EDGES if not o[2]]
 FIRST, DENSITY, ENERGY, SOURCE, SIGMA_1, LATE, SECOND, SIGMA_3 = range(8)
 N_GROUPS = 8
-EDGES = [(i, j, k) for i in (1, -1, 0) for j in (1, -1, 0) for k in (1, -1, 0) if abs(i) + abs(j) + abs(k) == 2]
 
 
 def face_state(z, a, b, c, d):
@@ -48,7 +50,7 @@
 
 
 def kernel(
-    sizes, q_hbm, g_hbm, adv, sig, pq, zq, sg, zs, src, zsrc, wt, sw, wb, sb, base, spd, rows_ref, lsem, ssem, rsem
+    sizes, q_hbm, g_hbm, adv, sig, pq, zq, sg, zs, src, zsrc, wt, sw, wb, sb, base, spd, rows_ref, pk, rk, lsem, ssem, rsem
 ):
     def peer(offset):
         out = {}
@@ -120,6 +122,46 @@
             group,
         )
 
+    narrow = lax.broadcasted_iota(jnp.int32, (1, 128), 1)
+
+    def place(start, step, layer, there):
+        if there:
+            return start - 1 - layer if step > 0 else start + 8 + layer
+        return start + 7 - layer if step > 0 else start + layer
+
+    def spot(offset, layer, i, there):
+        if offset[0]:
+            return place(PX, offset[0], layer, there), pl.ds(PY + i, 1)
+        return PX + i, pl.ds(place(PY, offset[1], layer, there), 1)
+
+    def turn(row, n):
+        return pltpu.roll(row, n % 128, 1) if n % 128 else row
+
+    def pack_lines(k, offsets, centre, depth):
+        for offset in offsets:
+            e = BESIDE.index(offset)
+            for layer in range(depth):
+                row = None
+                for i in range(8):
+                    x, r = spot(offset, layer, i, False)
+                    v = turn(centre[x, r, :], 16 * i + (16 if offset[2] > 0 else 0))
+                    row = v if row is None else jnp.where(narrow >= 16 * i, v, row)
+                pk[k, e, pl.ds(layer, 1), :] = row
+
+    def share_lines(group, k, offsets, depth):
+        for offset in offsets:
+            e = BESIDE.index(offset)
+            send(pk.at[k, e, pl.ds(0, depth), :], rk.at[k, e, pl.ds(0, depth), :], offset, group)
+
+    def spread_lines(k, lower, upper, depth):
+        for e, offset in enumerate(BESIDE):
+            target = lower if offset[2] > 0 else upper
+            for layer in range(depth):
+                row = rk[k, e, pl.ds(layer, 1), :]
+                for i in range(8):
+                    x, r = spot(offset, layer, i, True)
+                    target[x, r, :] = turn(row, -16 * i - (16 if offset[2] > 0 else 0))
+
     def sigma(s):
         return sg.at[s], zs.at[s, 0], zs.at[s, 1]
 
@@ -144,9 +186,11 @@
         inner = jnp.where(lane >= 64, here, upper)
         return jnp.where((lane >= 32) & (lane < 96), pltpu.roll(inner, 64, 1), outer)
 
+    pack_lines(0, BESIDE, pq.at[0], 2)
     arrived(FIRST)
-    for o in EDGES:
+    for o in DIAGONAL:
         share(DENSITY, o, *fields(0, 1), 0, 1)
+    share_lines(DENSITY, 0, BESIDE, 2)
     for o in FACES[:4]:
         share(DENSITY, o, *fields(0, 1), 1, 2)
     for o in FACES[4:]:
@@ -312,27 +356,27 @@
         lax.fori_loop(0, 8, body, 0)
 
     sources = (src, zsrc.at[0], zsrc.at[1])
-    far_edges = [o for o in EDGES if o[0]]
-    near_edges = [o for o in EDGES if not o[0]]
-    for planes, edges, faces in (((0, 7, 1, 6), far_edges, FACES[2:4]), ((2, 5, 3, 4), near_edges, FACES[:2] + FACES[4:])):
+    far_lines = [o for o in BESIDE if o[0]]
+    near_lines = [o for o in BESIDE if not o[0]]
+    for planes, lines, faces in (((0, 7, 1, 6), far_lines, FACES[2:4]), ((2, 5, 3, 4), near_lines, FACES[:2] + FACES[4:])):
         for i in planes:
             prepare(i)
         for i in planes:
             relax(0, i + PX, PY)
-        for o in edges:
-            share(SIGMA_1, o, *sigma(1), 0, 1)
+        if lines is far_lines:
+            for o in DIAGONAL:
+                share(SIGMA_1, o, *sigma(1), 0, 1)
+        pack_lines(1, lines, sg.at[1], 1)
+        share_lines(SIGMA_1, 1, lines, 1)
         for o in faces:
             share(SOURCE, o, *sources, 0, 1)
             share(SIGMA_1, o, *sigma(1), 0, 2)
     for o in FACES[:4]:
         share(LATE, o, *sources, 1, 2)
         share(LATE, o, *fields(0, 1), 2, 3)
-    for o in EDGES:
-        if o[2]:
-            share(LATE, o, *fields(0, 1), 1, 2)
-        else:
-            share(LATE, o, *fields(0, 1), 1, 2, 0, 1)
-            share(LATE, o, *fields(0, 1), 0, 1, 1, 2)
+    for o in DIAGONAL:
+        share(LATE, o, *fields(0, 1), 1, 2, 0, 1)
+        share(LATE, o, *fields(0, 1), 0, 1, 1, 2)
     for o in FACES[:4]:
         share(SECOND, o, *fields(1, 3), 1, 2)
         share(SECOND, o, *fields(4, 1), 0, 2)
@@ -340,19 +384,23 @@
     arrived(ENERGY)
     base_flux(2)
     arrived(DENSITY, SOURCE)
+    spread_lines(0, zq.at[0, 0], zq.at[1, 0], 2)
     widen(1)
     arrived(SIGMA_1)
+    spread_lines(1, zs.at[1, 0], zs.at[1, 1], 1)
     relax_wide(1, 1)
     for i in (0, 7, 1, 6, 2, 5):
         relax(2, i + PX, PY)
-    for o in far_edges:
+    for o in DIAGONAL:
         share(SIGMA_3, o, *sigma(3), 0, 2)
+    pack_lines(2, far_lines, sg.at[3], 2)
+    share_lines(SIGMA_3, 2, far_lines, 2)
     for o in FACES[2:4]:
         share(SIGMA_3, o, *sigma(3), 0, 3)
     for i in (3, 4):
         relax(2, i + PX, PY)
-    for o in near_edges:
-        share(SIGMA_3, o, *sigma(3), 0, 2)
+    pack_lines(2, near_lines, sg.at[3], 2)
+    share_lines(SIGMA_3, 2, near_lines, 2)
     for o in FACES[:2] + FACES[4:]:
         share(SIGMA_3, o, *sigma(3), 0, 3)
     arrived(LATE)
@@ -361,6 +409,7 @@
     base_flux(0)
     base_flux(1)
     arrived(SIGMA_3)
+    spread_lines(2, zs.at[3, 0], zs.at[3, 1], 2)
     relax_wide(3, 2)
 
     for i in range(8):
@@ -428,6 +477,8 @@
                 pltpu.VMEM((5, 8, 8, 128), f32),
                 pltpu.VMEM((12, 8, 8, 128), f32),
                 pltpu.VMEM((4096, 128), f32),
+                pltpu.VMEM((3, 8, 8, 128), f32),
+                pltpu.VMEM((3, 8, 8, 128), f32),
                 pltpu.SemaphoreType.DMA((2,)),
                 pltpu.SemaphoreType.DMA((1,)),
                 pltpu.SemaphoreType.DMA((N_GROUPS,)),

time: 38.8 us -> 37.4 us (0.964)
  Pallas kernels: 37.9 us -> 36.6 us
    pallas_call x1, Pallas kernels: 37.2 us -> 35.9 us  [on_device(): pl.pallas_call(functools.partial(kernel, sizes), out_shape=shapes, in_spe...]
where the time goes in v4:
time: 37.4 us; the launch traced here: 37.2 us
  Pallas kernels  36.6 us (98%)
  between operations  0.64 us (2%)
    pallas_call x1, Pallas kernels, on_device(): pl.pallas_call(functools.partial(kernel, sizes), out_shape=shapes, in_spe...  35.9 us

profile of v4, /device:TPU:1, one launch (start us, length us, event | category | flops | bytes accessed | tf_op | source)
XLA Modules:
  0.0 37.2 jit_solution(6966818666349736750)
XLA Ops:
  0.6 35.9 %shard_map.41 = (f32[5,8,8,128]{3,2,1,0:T(8,128)S(1)}, f32[8,8,128]{2,1,0:T(8,128)S(1)}) custom-call(f32[5,8,8,128]{3,2,1,0:T(8,128)} %q_hbm.1, f32[8,8,128]{2,1,0:T(8,128)} %g_hbm.1), custom_call_target="tpu_custom_call" | custom-call | tf_op jit(solution)/shard_map/pallas_call | solution.py:461
  36.5 0.7 %shard_map.42 = (f32[5,8,8,128]{3,2,1,0:T(8,128)}, f32[8,8,128]{2,1,0:T(8,128)}) custom-call(f32[5,8,8,128]{3,2,1,0:T(8,128)S(1)} %get-tuple-element.4.adv, f32[8,8,128]{2,1,0:T(8,128)S(1)} %get-tuple-element.5.sig), custom_call_target="tpu_custom_call" | custom-call | tf_op jit(solution)/shard_map/pallas_call | solution.py:488

commit v5 on v4

--- a/solution.py
+++ b/solution.py
@@ -366,11 +366,14 @@
         if lines is far_lines:
             for o in DIAGONAL:
                 share(SIGMA_1, o, *sigma(1), 0, 1)
-        pack_lines(1, lines, sg.at[1], 1)
-        share_lines(SIGMA_1, 1, lines, 1)
+            pack_lines(1, lines, sg.at[1], 1)
+            share_lines(SIGMA_1, 1, lines, 1)
         for o in faces:
             share(SOURCE, o, *sources, 0, 1)
             share(SIGMA_1, o, *sigma(1), 0, 2)
+        if lines is near_lines:
+            pack_lines(1, lines, sg.at[1], 1)
+            share_lines(SIGMA_1, 1, lines, 1)
     for o in FACES[:4]:
         share(LATE, o, *sources, 1, 2)
         share(LATE, o, *fields(0, 1), 2, 3)
@@ -399,10 +402,10 @@
         share(SIGMA_3, o, *sigma(3), 0, 3)
     for i in (3, 4):
         relax(2, i + PX, PY)
+    for o in FACES[:2] + FACES[4:]:
+        share(SIGMA_3, o, *sigma(3), 0, 3)
     pack_lines(2, near_lines, sg.at[3], 2)
     share_lines(SIGMA_3, 2, near_lines, 2)
-    for o in FACES[:2] + FACES[4:]:
-        share(SIGMA_3, o, *sigma(3), 0, 3)
     arrived(LATE)
     widen(2)
     arrived(SECOND)

time: 37.4 us -> 37.5 us (level)
  no operation moved by 1% of the time
where the time goes in v5:
time: 37.5 us; the launch traced here: 37.3 us
  Pallas kernels  36.7 us (98%)
  between operations  0.64 us (2%)
    pallas_call x1, Pallas kernels, on_device(): pl.pallas_call(functools.partial(kernel, sizes), out_shape=shapes, in_spe...  36 us

profile of v5, /device:TPU:1, one launch (start us, length us, event | category | flops | bytes accessed | tf_op | source)
XLA Modules:
  0.0 37.3 jit_solution(14555603376885775248)
XLA Ops:
  0.6 36.0 %shard_map.41 = (f32[5,8,8,128]{3,2,1,0:T(8,128)S(1)}, f32[8,8,128]{2,1,0:T(8,128)S(1)}) custom-call(f32[5,8,8,128]{3,2,1,0:T(8,128)} %q_hbm.1, f32[8,8,128]{2,1,0:T(8,128)} %g_hbm.1), custom_call_target="tpu_custom_call" | custom-call | tf_op jit(solution)/shard_map/pallas_call | solution.py:464
  36.6 0.7 %shard_map.42 = (f32[5,8,8,128]{3,2,1,0:T(8,128)}, f32[8,8,128]{2,1,0:T(8,128)}) custom-call(f32[5,8,8,128]{3,2,1,0:T(8,128)S(1)} %get-tuple-element.4.adv, f32[8,8,128]{2,1,0:T(8,128)S(1)} %get-tuple-element.5.sig), custom_call_target="tpu_custom_call" | custom-call | tf_op jit(solution)/shard_map/pallas_call | solution.py:491
